TPU v7x, 32 devices: a whole 2x2x4 slice. The times are simulated.
32 devices in a mesh: dp: 8 (over y, x, core), seq: 4 (over z).
Axes of the slice: x: 2, y: 2, z: 4, core: 2. Of those that a mesh axis runs over, the one named last changes fastest.
Arguments:
- tile_tokens: bfloat16 [8, 128, 3200], P('dp', 'seq'), may hold values from -6 to 6
- proj_weight: bfloat16 [3200, 8192], P('dp', 'seq')
- text_hidden: bfloat16 [8, 512, 8192], P('dp', 'seq'), may hold values from -6 to 6
- cotangent: bfloat16 [8, 512, 8192], P('dp', 'seq'), may hold values from -1.1953125 to 1.1953125
- norm_gain: float32 [8192], replicated, may hold values from 0.25 to 1.75
- placeholders: int32 [8, 128], P('dp'), may hold values from 0 to 511, as said below
- bucket_levels: int32 [8, 4, 3200], P('dp', 'seq'), may hold values from 2 to 16
- row_draws: float32 [8, 4, 3200], P('dp', 'seq'), may hold values from 0 to 1
- column_draws: float32 [8, 8192], P('dp', 'seq'), may hold values from 0 to 1
Outputs:
- weight_grad: float32 [3200, 8192], P('dp', 'seq')
- gain_grad: float32 [8192], replicated
Inputs may be any that keep to these rules, and one draw needn't show every extreme that they name: Each row is strictly increasing. Among the positions of one device's block of 128 positions stand at most 48 placeholders, and in every row some block holds exactly 48.
All inputs are finite; a program needn't handle non-finite values.
Results may differ from a plain program's by a relative error of at most 0.014.
Values may be sent and summed in bfloat16 or wider, within the bound.
No kernel may reach another device: no remote copies, remote signals or barrier semaphores. Data moves between devices by JAX's collectives and lax.ppermute only.
A program may use at most 64 MiB of HBM per device.

v0:
```python
import jax
import jax.numpy as jnp
from jax import lax
from jax.sharding import PartitionSpec as P

IMG_MOST = 48
EPSILON = 1e-06


def quantize(gradient, levels_now, rows_now, columns_now):
    bucket_norm = jnp.sqrt(jnp.sum(gradient * gradient, axis=1, keepdims=True) + EPSILON)
    step_count = levels_now.astype(jnp.float32)[:, None]
    offset = 0.25 + 0.25 * (rows_now[:, None] + columns_now[None, :])
    ratio = jnp.abs(gradient) / bucket_norm * step_count
    lower = jnp.floor(ratio)
    quantum = lower + jnp.clip(2.0 * (ratio - lower - offset) + 0.5, 0.0, 1.0)
    return jnp.sign(gradient) * bucket_norm * quantum / step_count


def on_device(
    tile_tokens,
    proj_weight,
    text_hidden,
    cotangent,
    norm_gain,
    placeholders,
    bucket_levels,
    row_draws,
    column_draws,
):
    seq_count = lax.axis_size("seq")
    seq_index = lax.axis_index("seq")
    replicas = lax.axis_size("dp")
    places = placeholders[0]
    image_total = places.shape[0]
    tok_rows = text_hidden.shape[1]
    model_width = text_hidden.shape[2]
    columns = proj_weight.shape[1]
    all_positions = tok_rows * seq_count
    zero_half = jnp.zeros((), jnp.bfloat16)
    own_text = text_hidden[0]
    own_cot = cotangent[0]
    gathered = lax.all_gather(tile_tokens[0], "seq", axis=0, tiled=True)
    patch_block = gathered
    embedded = jnp.dot(
        patch_block,
        lax.all_gather(proj_weight, "dp", axis=0, tiled=True),
        preferred_element_type=jnp.float32,
    ).astype(jnp.bfloat16)
    image_marks = jnp.zeros((all_positions,), jnp.int32).at[places].set(1)
    local_marks = lax.dynamic_slice_in_dim(image_marks, seq_index * tok_rows, tok_rows)
    is_image = local_marks[:, None] == 1
    owners = places // tok_rows
    owner_ids = jnp.arange(seq_count, dtype=jnp.int32)
    counts = jnp.sum((owners[:, None] == owner_ids[None, :]).astype(jnp.int32), axis=0)
    starts = jnp.cumsum(counts) - counts
    own_start = starts[seq_index]
    own_count = counts[seq_index]
    slot_ids = jnp.arange(IMG_MOST, dtype=jnp.int32)
    source_rows = jnp.clip(own_start + slot_ids, 0, image_total - 1)
    local_slots = jnp.clip(jnp.take(places, source_rows) - seq_index * tok_rows, 0, tok_rows - 1)
    slot_live = (slot_ids < own_count)[:, None]
    flat_index = owners * IMG_MOST + (
        jnp.arange(image_total, dtype=jnp.int32) - jnp.take(starts, owners)
    )
    outgoing = jnp.where(slot_live, jnp.take(own_cot, local_slots, axis=0), zero_half)
    returned = lax.all_to_all(outgoing[None], "seq", split_axis=2, concat_axis=0, tiled=True)
    image_cot = jnp.take(returned.reshape(-1, columns), flat_index, axis=0).astype(jnp.float32)
    emb_float = embedded.astype(jnp.float32)
    column_gain = lax.dynamic_slice_in_dim(norm_gain, seq_index * columns, columns)
    grad_in = image_cot * column_gain[None, :]
    squares, mixed = lax.psum(
        (jnp.sum(emb_float * emb_float, axis=1), jnp.sum(grad_in * emb_float, axis=1)), "seq"
    )
    inverse = lax.rsqrt(squares / model_width + EPSILON)[:, None]
    normed = emb_float * inverse
    emb_grad = ((grad_in - normed * (mixed[:, None] * inverse / model_width)) * inverse).astype(
        jnp.bfloat16
    )
    image_part = jnp.sum(image_cot * normed, axis=0)
    text_float = own_text.astype(jnp.float32)
    text_inverse = lax.rsqrt(jnp.mean(text_float * text_float, axis=1, keepdims=True) + EPSILON)
    text_terms = own_cot.astype(jnp.float32) * text_float * text_inverse
    text_part = jnp.sum(jnp.where(is_image, 0.0, text_terms), axis=0)
    placed_part = lax.dynamic_update_slice_in_dim(
        jnp.zeros((model_width,), jnp.float32), image_part, seq_index * columns, 0
    )
    gain_part = text_part + placed_part
    own_levels = bucket_levels[0, 0]
    own_row_draws = row_draws[0, 0]
    own_column_draws = column_draws[0]
    patch_block = gathered
    gradient = lax.dot_general(
        patch_block, emb_grad, (((0,), (0,)), ((), ())), preferred_element_type=jnp.float32
    )
    summed = lax.psum_scatter(
        quantize(gradient, own_levels, own_row_draws, own_column_draws).astype(jnp.bfloat16),
        "dp",
        scatter_dimension=0,
        tiled=True,
    ).astype(jnp.float32)
    gain_total = lax.psum(gain_part, ("dp", "seq"))
    return (summed / replicas, gain_total / replicas)


def solution(mesh):
    return jax.shard_map(
        on_device,
        mesh=mesh,
        in_specs=(
            P("dp", "seq", None),
            P("dp", "seq"),
            P("dp", "seq", None),
            P("dp", "seq", None),
            P(),
            P("dp", None),
            P("dp", "seq", None),
            P("dp", "seq", None),
            P("dp", "seq"),
        ),
        out_specs=(P("dp", "seq"), P()),
        check_vma=False,
    )
```

profile of v0, /device:TPU:0, one launch (start us, length us, event | category | flops | bytes accessed | tf_op | source)
XLA Modules:
  0.0 315.0 jit_solution(2458585537406789046)
XLA Ops:
  7.3 0.7 all-gather.3.cloned.1.call-update
  7.9 0.7 and_select_fusion.5
  9.5 0.7 fusion.34
  10.2 0.7 fusion.33
  10.9 1.4 gather_fusion
  12.3 0.7 fusion.31
  13.0 3.6 %gather_fusion.1 = bf16[48,8192]{1,0:T(8,128)(2,1)S(1)} fusion(bf16[128,8192]{1,0:T(8,128)(2,1)} %bitcast.74, s32[1024]{0:T(1024)S(1)} %pad_clamp_fusion.1), kind=kCustom, calls=%fused_computation.1 | custom fusion | bytes 1573056 | tf_op jit(solution)/shard_map/jit(_take)/gather | solution.py:66
  16.6 1.3 compare_and_fusion
  18.1 6.8 %copy.22 = bf16[1,48,8192]{1,0,2:T(2,128)(2,1)} copy(bf16[1,48,8192]{2,1,0:T(8,128)(2,1)S(1)} %fusion.21) | data formatting | bytes 1572864 | tf_op jit(solution)/shard_map/jit(_where)/select_n | solution.py:66
  25.3 45.2 %reduce.4 = bf16[8192,48]{1,0:T(8,128)(2,1)S(1)} reduce(bf16[8192,1,48]{2,1,0:T(2,128)(2,1)} %bitcast.76, bf16[]{:T(256)} %broadcast.575), dimensions={1}, to_apply=%bitcast.63.reduce_sub_computation | reduce | bytes 1572866
  70.6 4.0 %reshape.423 = bf16[4,2,49152]{2,1,0:T(2,128)(2,1)} reshape(bf16[8192,48]{1,0:T(8,128)(2,1)S(1)} %reduce.4) | data formatting | bytes 1572864
  74.6 6.3 %all-to-all-start = ((bf16[4,2,49152]{2,1,0:T(2,128)(2,1)}), bf16[4,2,49152]{2,1,0:T(2,128)(2,1)S(1)}, u32[]{:S(2)}, u32[]{:S(2)}) async-start(bf16[4,2,49152]{2,1,0:T(2,128)(2,1)} %reshape.423), calls=%async_computation | async-start | bytes 1572864 | tf_op jit(solution)/shard_map/all_to_all | solution.py:67
  80.9 0.7 dynamic_slice.14
  81.7 2.6 compare_and_fusion.1
  84.4 30.7 %all-gather = bf16[1,128,3200]{2,1,0:T(8,128)(2,1)S(1)} all-gather(bf16[1,32,3200]{2,1,0:T(8,128)(2,1)S(1)} %copy-done.4), channel_id=2, replica_groups=mesh['dp'=8,'seq'=4] {'seq'}, dimensions={1}, use_global_device_ids=true | all-gather | bytes 1024000 | tf_op jit(solution)/shard_map/all_gather | solution.py:43
  115.0 4.6 %reshape.424 = bf16[8192,1,48]{2,1,0:T(2,128)(2,1)} reshape(bf16[4,2,49152]{2,1,0:T(2,128)(2,1)S(1)} %all-to-all-done) | data formatting | bytes 1572864
  119.6 8.1 %copy.23 = bf16[1,48,8192]{2,1,0:T(8,128)(2,1)S(1)} copy(bf16[1,48,8192]{1,0,2:T(2,128)(2,1)} %bitcast.77) | data formatting | bytes 1572864 | tf_op jit(solution)/shard_map/all_to_all | solution.py:67
  128.8 0.9 gather_fusion.2
  129.8 7.1 %multiply_reduce_fusion.1 = (f32[128]{0:T(128)S(1)}, f32[128,2048]{1,0:T(8,128)S(1)}) fusion(bf16[3200,2048]{1,0:T(8,128)(2,1)} %all-gather.3.cloned.1.call-done, bf16[1,128,3200]{2,1,0:T(8,128)(2,1)S(1)} %all-gather), kind=kOutput, calls=%fused_computation.31 | convolution fusion | flops 1678770048 | bytes 14975488 | tf_op jit(solution)/shard_map/dot_general | solution.py:45
  136.9 11.1 %psum.21 = f32[128]{0:T(128)S(1)} all-reduce(f32[128]{0:T(128)S(1)} %get-tuple-element.22), channel_id=1, replica_groups=mesh['dp'=8,'seq'=4] {'seq'}, use_global_device_ids=true, to_apply=%region_3.4 | all-reduce | flops 128 | bytes 1024 | tf_op jit(solution)/shard_map/psum | solution.py:72
  148.4 8.4 %psum.22 = f32[128]{0:T(128)S(1)} all-reduce(f32[128]{0:T(128)S(1)} %get-tuple-element.13), channel_id=1, replica_groups=mesh['dp'=8,'seq'=4] {'seq'}, use_global_device_ids=true, to_apply=%region_5.6 | all-reduce | flops 128 | bytes 1024 | tf_op jit(solution)/shard_map/psum | solution.py:72
  156.8 5.1 %multiply_reduce_fusion = (f32[3200]{0:T(1024)S(1)}, f32[2048,3200]{1,0:T(8,128)S(1)}) fusion(bf16[1,128,3200]{2,1,0:T(8,128)(2,1)S(1)} %all-gather, f32[128,2048]{1,0:T(8,128)} %copy-done.2, f32[128]{0:T(128)S(1)} %multiply_multiply_fusion, f32[128]{0:T(128)S(1)} %add_rsqrt_fusion.1, f32[2048]{0:T(1024)S(1)} %dynamic_slice.14, ...), kind=kOutput, calls=%fused_computation.12 | convolution fusion | flops 1692922752 | bytes 28628608 | tf_op jit(solution)/shard_map/dot_general | solution.py:93
  162.0 22.2 %fusion.6 = bf16[3200,2048]{0,1:T(8,128)(2,1)} fusion(f32[2048,3200]{1,0:T(8,128)S(1)} %get-tuple-element.25, f32[3200]{0:T(1024)S(1)} %convert_reduce_fusion, f32[2048]{0:T(1024)S(1)} %bitcast.79, f32[3200]{0:T(1024)S(1)} %reduce.2, f32[3200]{0:T(1024)S(1)} %add_sqrt_fusion), kind=kLoop, calls=%fused_computation.13 | loop fusion | flops 117964800 | bytes 39368192 | tf_op jit(solution)/shard_map/convert_element_type | solution.py:97
  184.1 18.3 %copy.26 = bf16[3200,2048]{1,0:T(8,128)(2,1)} copy(bf16[3200,2048]{0,1:T(8,128)(2,1)} %fusion.6) | data formatting | bytes 26214400
  202.5 1.0 scatter_custom_fusion
  203.6 2.1 fusion.10
  205.7 2.6 fusion.9
  208.3 41.3 %psum.23 = f32[8192]{0:T(1024)S(1)} all-reduce(f32[8192]{0:T(1024)S(1)} %add_dynamic-update-slice_fusion), channel_id=1, replica_groups=mesh['dp'=8,'seq'=4] {'dp','seq'}, use_global_device_ids=true, to_apply=%region_12.13 | all-reduce | flops 8192 | bytes 65536 | tf_op jit(solution)/shard_map/psum | solution.py:102
  250.3 47.4 %reduce-scatter.4.cloned.1.call-done = bf16[400,2048]{1,0:T(8,128)(2,1)} async-done(((bf16[3200,2048]{1,0:T(8,128)(2,1)}), bf16[400,2048]{1,0:T(8,128)(2,1)}) %reduce-scatter.4.cloned.1.call-update) | async-done | bytes 1638416
  297.7 2.8 copy.27
  300.5 2.5 convert_multiply_fusion.2
  303.0 5.2 %copy.25 = f32[400,2048]{1,0:T(8,128)} copy(f32[400,2048]{0,1:T(8,128)} %convert_multiply_fusion.2) | data formatting | bytes 6553600
  (45 shorter events, 4.0 us)
Async XLA Ops:
  7.2 74.5 %copy-start = (s32[1,128]{1,0:T(1,128)S(1)}, s32[1,128]{1,0:T(1,128)}, u32[]{:S(2)}) copy-start(s32[1,128]{1,0:T(1,128)} %param.14) | copy-start | bytes 1540
  7.2 74.5 %copy-start.6 = (f32[1,1,3200]{2,1,0:T(1,128)S(1)}, f32[1,1,3200]{2,1,0:T(1,128)}, u32[]{:S(2)}) copy-start(f32[1,1,3200]{2,1,0:T(1,128)} %param.16) | copy-start | bytes 38404
  7.2 77.1 %copy-start.5 = (s32[1,1,3200]{2,1,0:T(1,128)S(1)}, s32[1,1,3200]{2,1,0:T(1,128)}, u32[]{:S(2)}) copy-start(s32[1,1,3200]{2,1,0:T(1,128)} %param.15) | copy-start | bytes 38404
  7.2 77.2 %copy-start.4 = (bf16[1,32,3200]{2,1,0:T(8,128)(2,1)S(1)}, bf16[1,32,3200]{2,1,0:T(8,128)(2,1)}, u32[]{:S(2)}) copy-start(bf16[1,32,3200]{2,1,0:T(8,128)(2,1)} %param.9) | copy-start | bytes 614404
  7.2 122.6 %all-gather.3.cloned.1.call-start = ((), (), s32[]{:S(2)}) async-start(), calls=%async_computation.2 | async-start | bytes 14745600 | tf_op jit(solution)/shard_map/all_gather | solution.py:47
  74.6 40.5 %all-to-all-start = ((bf16[4,2,49152]{2,1,0:T(2,128)(2,1)}), bf16[4,2,49152]{2,1,0:T(2,128)(2,1)S(1)}, u32[]{:S(2)}, u32[]{:S(2)}) async-start(bf16[4,2,49152]{2,1,0:T(2,128)(2,1)} %reshape.423), calls=%async_computation | async-start | bytes 1572864 | tf_op jit(solution)/shard_map/all_to_all | solution.py:67
  80.9 216.8 %reduce-scatter.4.cloned.1.call-start = ((), (), s32[]{:S(2)}) async-start(), calls=%async_computation.3 | async-start | bytes 14745600
  129.7 27.0 %copy-start.3 = (bf16[128,2048]{1,0:T(8,128)(2,1)}, bf16[128,2048]{1,0:T(8,128)(2,1)S(1)}, u32[]{:S(2)}) copy-start(bf16[128,2048]{1,0:T(8,128)(2,1)S(1)} %gather_fusion.2) | copy-start | bytes 1572868
  136.8 19.9 %copy-start.2 = (f32[128,2048]{1,0:T(8,128)}, f32[128,2048]{1,0:T(8,128)S(1)}, u32[]{:S(2)}) copy-start(f32[128,2048]{1,0:T(8,128)S(1)} %get-tuple-element.23) | copy-start | bytes 3145732
  156.8 5.2 %copy-start.7 = (f32[1,2048]{1,0:T(1,128)S(1)}, f32[1,2048]{1,0:T(1,128)}, u32[]{:S(2)}) copy-start(f32[1,2048]{1,0:T(1,128)} %param.17) | copy-start | bytes 24580
  202.5 3.2 %copy-start.1 = (bf16[1,128,8192]{2,1,0:T(8,128)(2,1)S(1)}, bf16[1,128,8192]{2,1,0:T(8,128)(2,1)}, u32[]{:S(2)}) copy-start(bf16[1,128,8192]{2,1,0:T(8,128)(2,1)} %param.12) | copy-start | bytes 6291460
Sparse Core Ops, SparseCore 0:
  9.9 76.9 all-gather.2
  202.6 95.0 reduce-scatter.3
where the time goes:
time: 316 us; the launch traced here: 315 us
  blocking collectives  91.5 us (29%)
  other arithmetic  82.2 us (26%)
  local copies, waits for them, and re-layouts  60.3 us (19%)
  waiting for transfers between devices  48.1 us (15%)
  between operations  14.3 us (5%)
  matrix products  12.2 us (4%)
  starting transfers between devices  6.39 us (2%)
    unnamed x3, waiting for transfers between devices  48.1 us
    unnamed x2, other arithmetic  45.3 us
    psum x1, blocking collectives, on_device(): gain_total = lax.psum(gain_part, ('dp', 'seq'))  41.3 us
    unnamed x22, local copies, waits for them, and re-layouts  35.4 us
    all_gather x1, blocking collectives, on_device(): gathered = lax.all_gather(tile_tokens[0], 'seq', axis=0, tiled=True)  30.7 us
    convert_element_type x1, other arithmetic, on_device(): quantize(gradient, own_levels, own_row_draws, own_column_draws)  22.2 us
    psum x2, blocking collectives, on_device(): lax.psum((jnp.sum(emb_float * emb_float, axis=1), jnp.sum(grad_in * emb_f...  19.5 us
    all_to_all x3, local copies, waits for them, and re-layouts, on_device(): lax.all_to_all(outgoing[None], 'seq', split_axis=2, concat_axis=0, tiled=...  9.14 us
  transfers between devices with their start and end apart: 3, of which 1 were waited for; matrix products, arithmetic and copies ran while one was open for 29% of the time, Pallas kernels for 0%

commit v1 on v0

--- a/solution.py
+++ b/solution.py
@@ -99,7 +99,7 @@
         scatter_dimension=0,
         tiled=True,
     ).astype(jnp.float32)
-    gain_total = lax.psum(gain_part, ("dp", "seq"))
+    gain_total = lax.psum(lax.psum(gain_part, axis_name="seq"), axis_name="dp")
     return (summed / replicas, gain_total / replicas)
 
 

time: 316 us -> 333 us (1.054)
  waiting for transfers between devices: 48.1 us -> 71.9 us
  blocking collectives: 91.5 us -> 77.4 us
  local copies, waits for them, and re-layouts: 60.3 us -> 64.8 us
    unnamed x3, waiting for transfers between devices: 48.1 us -> 71.8 us
    psum x1, blocking collectives: 41.3 us -> 22.3 us  [on_device(): gain_total = lax.psum(lax.psum(gain_part, axis_name='seq'), axis_name='dp')]
    psum x2, blocking collectives: 19.5 us -> 27.6 us  [on_device(): lax.psum((jnp.sum(emb_float * emb_float, axis=1), jnp.sum(grad_in * emb_f...]
where the time goes in v1:
time: 333 us; the launch traced here: 331 us
  other arithmetic  84 us (25%)
  blocking collectives  77.4 us (23%)
  waiting for transfers between devices  71.9 us (22%)
  local copies, waits for them, and re-layouts  64.8 us (19%)
  between operations  14.3 us (4%)
  matrix products  12 us (4%)
  starting transfers between devices  6.49 us (2%)
    unnamed x3, waiting for transfers between devices  71.8 us
    unnamed x2, other arithmetic  46.5 us
    unnamed x22, local copies, waits for them, and re-layouts  37.7 us
    psum x2, blocking collectives, on_device(): lax.psum((jnp.sum(emb_float * emb_float, axis=1), jnp.sum(grad_in * emb_f...  27.6 us
    all_gather x1, blocking collectives, on_device(): gathered = lax.all_gather(tile_tokens[0], 'seq', axis=0, tiled=True)  27.5 us
    psum x1, blocking collectives, on_device(): gain_total = lax.psum(lax.psum(gain_part, axis_name='seq'), axis_name='dp')  22.3 us
    convert_element_type x1, other arithmetic, on_device(): quantize(gradient, own_levels, own_row_draws, own_column_draws)  22.1 us
    all_to_all x3, local copies, waits for them, and re-layouts, on_device(): lax.all_to_all(outgoing[None], 'seq', split_axis=2, concat_axis=0, tiled=...  9.14 us
  transfers between devices with their start and end apart: 3, of which 1 were waited for; matrix products, arithmetic and copies ran while one was open for 29% of the time, Pallas kernels for 0%

profile of v1, /device:TPU:0, one launch (start us, length us, event | category | flops | bytes accessed | tf_op | source)
XLA Modules:
  0.0 330.9 jit_solution(4915978098089223868)
XLA Ops:
  7.2 0.7 all-gather.3.cloned.1.call-update
  7.9 0.7 and_select_fusion.5
  10.2 0.7 fusion.33
  10.8 1.4 gather_fusion
  12.3 0.7 fusion.31
  13.0 3.8 %gather_fusion.1 = bf16[48,8192]{1,0:T(8,128)(2,1)S(1)} fusion(bf16[128,8192]{1,0:T(8,128)(2,1)} %bitcast.75, s32[1024]{0:T(1024)S(1)} %pad_clamp_fusion.1), kind=kCustom, calls=%fused_computation.1 | custom fusion | bytes 1573056 | tf_op jit(solution)/shard_map/jit(_take)/gather | solution.py:66
  16.8 1.3 compare_and_fusion
  18.0 1.0 fusion.21
  19.1 8.9 %copy.22 = bf16[1,48,8192]{1,0,2:T(2,128)(2,1)} copy(bf16[1,48,8192]{2,1,0:T(8,128)(2,1)} %fusion.21) | data formatting | bytes 1572864 | tf_op jit(solution)/shard_map/jit(_where)/select_n | solution.py:66
  28.5 46.5 %reduce.4 = bf16[8192,48]{1,0:T(8,128)(2,1)} reduce(bf16[8192,1,48]{2,1,0:T(2,128)(2,1)} %bitcast.77, bf16[]{:T(256)} %broadcast.575), dimensions={1}, to_apply=%bitcast.63.reduce_sub_computation | reduce | bytes 1572866
  74.9 5.1 %reshape.423 = bf16[4,2,49152]{2,1,0:T(2,128)(2,1)} reshape(bf16[8192,48]{1,0:T(8,128)(2,1)} %reduce.4) | data formatting | bytes 1572864
  80.0 6.5 %all-to-all-start = ((bf16[4,2,49152]{2,1,0:T(2,128)(2,1)}), bf16[4,2,49152]{2,1,0:T(2,128)(2,1)}, u32[]{:S(2)}, u32[]{:S(2)}) async-start(bf16[4,2,49152]{2,1,0:T(2,128)(2,1)} %reshape.423), calls=%async_computation | async-start | bytes 1572864 | tf_op jit(solution)/shard_map/all_to_all | solution.py:67
  86.5 1.0 scatter_custom_fusion
  87.5 2.5 compare_and_fusion.1
  90.1 0.7 dynamic_slice.14
  90.9 2.1 fusion.10
  93.0 27.5 %all-gather = bf16[1,128,3200]{2,1,0:T(8,128)(2,1)S(1)} all-gather(bf16[1,32,3200]{2,1,0:T(8,128)(2,1)S(1)} %copy-done.4), channel_id=2, replica_groups=mesh['dp'=8,'seq'=4] {'seq'}, dimensions={1}, use_global_device_ids=true | all-gather | bytes 1024000 | tf_op jit(solution)/shard_map/all_gather | solution.py:43
  120.5 2.5 fusion.9
  123.0 5.8 %reshape.424 = bf16[8192,1,48]{2,1,0:T(2,128)(2,1)} reshape(bf16[4,2,49152]{2,1,0:T(2,128)(2,1)} %all-to-all-done) | data formatting | bytes 1572864
  128.8 8.1 %copy.23 = bf16[1,48,8192]{2,1,0:T(8,128)(2,1)S(1)} copy(bf16[1,48,8192]{1,0,2:T(2,128)(2,1)} %bitcast.78) | data formatting | bytes 1572864 | tf_op jit(solution)/shard_map/all_to_all | solution.py:67
  137.9 0.9 gather_fusion.2
  138.9 6.9 %multiply_reduce_fusion.1 = (f32[128]{0:T(128)S(1)}, f32[128,2048]{1,0:T(8,128)S(1)}) fusion(bf16[3200,2048]{1,0:T(8,128)(2,1)} %all-gather.3.cloned.1.call-done, bf16[1,128,3200]{2,1,0:T(8,128)(2,1)S(1)} %all-gather), kind=kOutput, calls=%fused_computation.31 | convolution fusion | flops 1678770048 | bytes 14975488 | tf_op jit(solution)/shard_map/dot_general | solution.py:45
  145.8 11.2 %psum.28 = f32[128]{0:T(128)S(1)} all-reduce(f32[128]{0:T(128)S(1)} %get-tuple-element.24), channel_id=1, replica_groups=mesh['dp'=8,'seq'=4] {'seq'}, use_global_device_ids=true, to_apply=%region_3.4 | all-reduce | flops 128 | bytes 1024 | tf_op jit(solution)/shard_map/psum | solution.py:72
  157.4 16.4 %all-reduce = (f32[128]{0:T(128)S(1)}, f32[8192]{0:T(1024)S(1)}) all-reduce(f32[128]{0:T(128)S(1)} %get-tuple-element.13, f32[8192]{0:T(1024)S(1)} %add_dynamic-update-slice_fusion), channel_id=1, replica_groups=mesh['dp'=8,'seq'=4] {'seq'}, use_global_device_ids=true, to_apply=%region_5.6 | all-reduce | flops 8320 | bytes 66560 | tf_op jit(solution)/shard_map/psum | solution.py:72
  173.9 5.1 %multiply_reduce_fusion = (f32[3200]{0:T(1024)S(1)}, f32[2048,3200]{1,0:T(8,128)S(1)}) fusion(bf16[1,128,3200]{2,1,0:T(8,128)(2,1)S(1)} %all-gather, f32[128,2048]{1,0:T(8,128)} %copy-done.2, f32[128]{0:T(128)S(1)} %multiply_multiply_fusion, f32[128]{0:T(128)S(1)} %add_rsqrt_fusion.1, f32[2048]{0:T(1024)S(1)} %dynamic_slice.14, ...), kind=kOutput, calls=%fused_computation.12 | convolution fusion | flops 1692922752 | bytes 28628608 | tf_op jit(solution)/shard_map/dot_general | solution.py:93
  179.1 22.1 %fusion.6 = bf16[3200,2048]{0,1:T(8,128)(2,1)} fusion(f32[2048,3200]{1,0:T(8,128)S(1)} %get-tuple-element.27, f32[3200]{0:T(1024)S(1)} %convert_reduce_fusion, f32[2048]{0:T(1024)S(1)} %bitcast.80, f32[3200]{0:T(1024)S(1)} %reduce.2, f32[3200]{0:T(1024)S(1)} %add_sqrt_fusion), kind=kLoop, calls=%fused_computation.13 | loop fusion | flops 117964800 | bytes 39368192 | tf_op jit(solution)/shard_map/convert_element_type | solution.py:97
  201.2 18.3 %copy.26 = bf16[3200,2048]{1,0:T(8,128)(2,1)} copy(bf16[3200,2048]{0,1:T(8,128)(2,1)} %fusion.6) | data formatting | bytes 26214400
  219.5 22.3 %psum.31 = f32[8192]{0:T(1024)S(1)} all-reduce(f32[8192]{0:T(1024)S(1)} %get-tuple-element.15), channel_id=1, replica_groups=mesh['dp'=8,'seq'=4] {'dp'}, use_global_device_ids=true, to_apply=%region_13.14 | all-reduce | flops 8192 | bytes 65536 | tf_op jit(solution)/shard_map/psum | solution.py:102
  242.5 71.1 %reduce-scatter.4.cloned.1.call-done = bf16[400,2048]{1,0:T(8,128)(2,1)} async-done(((bf16[3200,2048]{1,0:T(8,128)(2,1)}), bf16[400,2048]{1,0:T(8,128)(2,1)}) %reduce-scatter.4.cloned.1.call-update) | async-done | bytes 1638416
  313.6 2.8 copy.27
  316.4 2.5 convert_multiply_fusion.2
  318.9 5.2 %copy.25 = f32[400,2048]{1,0:T(8,128)} copy(f32[400,2048]{0,1:T(8,128)} %convert_multiply_fusion.2) | data formatting | bytes 6553600
  (45 shorter events, 4.5 us)
Async XLA Ops:
  7.2 79.3 %copy-start = (s32[1,128]{1,0:T(1,128)S(1)}, s32[1,128]{1,0:T(1,128)}, u32[]{:S(2)}) copy-start(s32[1,128]{1,0:T(1,128)} %param.14) | copy-start | bytes 1540
  7.2 82.8 %copy-start.5 = (s32[1,1,3200]{2,1,0:T(1,128)S(1)}, s32[1,1,3200]{2,1,0:T(1,128)}, u32[]{:S(2)}) copy-start(s32[1,1,3200]{2,1,0:T(1,128)} %param.15) | copy-start | bytes 38404
  7.2 83.6 %copy-start.6 = (f32[1,1,3200]{2,1,0:T(1,128)S(1)}, f32[1,1,3200]{2,1,0:T(1,128)}, u32[]{:S(2)}) copy-start(f32[1,1,3200]{2,1,0:T(1,128)} %param.16) | copy-start | bytes 38404
  7.2 131.7 %all-gather.3.cloned.1.call-start = ((), (), s32[]{:S(2)}) async-start(), calls=%async_computation.2 | async-start | bytes 14745600 | tf_op jit(solution)/shard_map/all_gather | solution.py:47
  13.0 80.0 %copy-start.4 = (bf16[1,32,3200]{2,1,0:T(8,128)(2,1)S(1)}, bf16[1,32,3200]{2,1,0:T(8,128)(2,1)}, u32[]{:S(2)}) copy-start(bf16[1,32,3200]{2,1,0:T(8,128)(2,1)} %param.9) | copy-start | bytes 614404
  13.0 107.5 %copy-start.1 = (bf16[1,128,8192]{2,1,0:T(8,128)(2,1)S(1)}, bf16[1,128,8192]{2,1,0:T(8,128)(2,1)}, u32[]{:S(2)}) copy-start(bf16[1,128,8192]{2,1,0:T(8,128)(2,1)} %param.12) | copy-start | bytes 6291460
  80.0 42.9 %all-to-all-start = ((bf16[4,2,49152]{2,1,0:T(2,128)(2,1)}), bf16[4,2,49152]{2,1,0:T(2,128)(2,1)}, u32[]{:S(2)}, u32[]{:S(2)}) async-start(bf16[4,2,49152]{2,1,0:T(2,128)(2,1)} %reshape.423), calls=%async_computation | async-start | bytes 1572864 | tf_op jit(solution)/shard_map/all_to_all | solution.py:67
  86.5 227.1 %reduce-scatter.4.cloned.1.call-start = ((), (), s32[]{:S(2)}) async-start(), calls=%async_computation.3 | async-start | bytes 14745600
  138.9 35.0 %copy-start.3 = (bf16[128,2048]{1,0:T(8,128)(2,1)}, bf16[128,2048]{1,0:T(8,128)(2,1)S(1)}, u32[]{:S(2)}) copy-start(bf16[128,2048]{1,0:T(8,128)(2,1)S(1)} %gather_fusion.2) | copy-start | bytes 1572868
  145.8 28.1 %copy-start.2 = (f32[128,2048]{1,0:T(8,128)}, f32[128,2048]{1,0:T(8,128)S(1)}, u32[]{:S(2)}) copy-start(f32[128,2048]{1,0:T(8,128)S(1)} %get-tuple-element.25) | copy-start | bytes 3145732
  173.9 5.2 %copy-start.7 = (f32[1,2048]{1,0:T(1,128)S(1)}, f32[1,2048]{1,0:T(1,128)}, u32[]{:S(2)}) copy-start(f32[1,2048]{1,0:T(1,128)} %param.17) | copy-start | bytes 24580
Sparse Core Ops, SparseCore 0:
  9.9 76.9 all-gather.2
  219.7 93.9 reduce-scatter.3
